TPU v7x, 32 devices: a whole 2x2x4 slice. The times are simulated.
32 devices in a mesh: fsdp: 2 (over y), trow: 4 (over x, core), tcol: 4 (over z).
Axes of the slice: x: 2, y: 2, z: 4, core: 2. Of those that a mesh axis runs over, the one named last changes fastest.
Arguments:
- tokens: bfloat16 [512, 4096], P('fsdp', 'tcol'), may hold values from -100 to 100
- w_up: bfloat16 [4096, 16384], P('tcol', ('fsdp', 'trow')), may hold values from -0.1875 to 0.1875
- w_down: bfloat16 [16384, 4096], P(('fsdp', 'trow'), 'tcol'), may hold values from -0.046875 to 0.046875
- cotangent: bfloat16 [512, 4096], P('fsdp', 'tcol'), may hold values from -6 to 6
Outputs:
- mixed: bfloat16 [512, 4096], P('fsdp', 'tcol')
- input_gradient: bfloat16 [512, 4096], P('fsdp', 'tcol')
- grad_up: bfloat16 [4096, 16384], P('tcol', ('fsdp', 'trow'))
- grad_down: bfloat16 [16384, 4096], P(('fsdp', 'trow'), 'tcol')
All inputs are finite; a program needn't handle non-finite values.
Results may differ from a plain program's by a relative error of at most 0.02.
Values may be sent and summed in bfloat16 or wider, within the bound.
No kernel may reach another device: no remote copies, remote signals or barrier semaphores. Data moves between devices by JAX's collectives and lax.ppermute only.
A program may use at most 128 MiB of HBM per device.

v0:
```python
import jax
import jax.numpy as jnp
from jax import lax
from jax.sharding import PartitionSpec as P


def gelu_value(pre):
    phi = 0.5 * (1.0 + jax.scipy.special.erf(pre * 0.7071067811865476))
    return pre * phi


def gelu_slope(pre):
    phi = 0.5 * (1.0 + jax.scipy.special.erf(pre * 0.7071067811865476))
    return phi + pre * jnp.exp(-0.5 * pre * pre) * 0.3989422804014327


def contract(left, right, left_dim, right_dim):
    return lax.dot_general(
        left, right, (((left_dim,), (right_dim,)), ((), ())), preferred_element_type=jnp.float32
    )


def local(tokens, w_up, w_down, cotangent):
    width = tokens.shape[1] * lax.axis_size("tcol")
    input_float = tokens.astype(jnp.float32)
    cot_all = lax.all_gather(cotangent, "fsdp", axis=0, tiled=True)
    sum_one, sum_two = lax.psum(
        (jnp.sum(input_float, axis=1), jnp.sum(input_float * input_float, axis=1)), "tcol"
    )
    token_mean = sum_one / width
    var = sum_two / width - token_mean * token_mean
    inverse_stddev = lax.rsqrt(var + 1e-05)
    centered_scaled = (input_float - token_mean[:, None]) * inverse_stddev[:, None]
    normed = lax.all_gather(centered_scaled.astype(jnp.bfloat16), "fsdp", axis=0, tiled=True)
    dhid = lax.psum(contract(cot_all, w_down, 1, 1).astype(jnp.bfloat16), "tcol").astype(
        jnp.float32
    )
    pre = lax.psum(contract(normed, w_up, 1, 0).astype(jnp.bfloat16), "tcol").astype(jnp.float32)
    hidden = gelu_value(pre).astype(jnp.bfloat16)
    dpre = (dhid * gelu_slope(pre)).astype(jnp.bfloat16)
    branch = lax.psum_scatter(
        contract(hidden, w_down, 1, 0).astype(jnp.bfloat16), "fsdp", scatter_dimension=0, tiled=True
    )
    branch = lax.psum(branch, "trow").astype(jnp.float32)
    mixed = (input_float + branch).astype(jnp.bfloat16)
    dnorm = lax.psum_scatter(
        contract(dpre, w_up, 1, 1).astype(jnp.bfloat16), "fsdp", scatter_dimension=0, tiled=True
    )
    dnorm = lax.psum(dnorm, "trow").astype(jnp.float32)
    grad_down = contract(hidden, cot_all, 0, 0).astype(jnp.bfloat16)
    grad_up = contract(normed, dpre, 0, 0).astype(jnp.bfloat16)
    mean_first, mean_second = lax.psum(
        (jnp.sum(dnorm, axis=1), jnp.sum(dnorm * centered_scaled, axis=1)), "tcol"
    )
    first_moment = mean_first / width
    second_moment = mean_second / width
    input_gradient = cotangent.astype(jnp.float32) + inverse_stddev[:, None] * (
        dnorm - first_moment[:, None] - centered_scaled * second_moment[:, None]
    )
    return (mixed, input_gradient.astype(jnp.bfloat16), grad_up, grad_down)


def solution(mesh):
    return jax.shard_map(
        local,
        mesh=mesh,
        in_specs=(
            P("fsdp", "tcol"),
            P("tcol", ("fsdp", "trow")),
            P(("fsdp", "trow"), "tcol"),
            P("fsdp", "tcol"),
        ),
        out_specs=(
            P("fsdp", "tcol"),
            P("fsdp", "tcol"),
            P("tcol", ("fsdp", "trow")),
            P(("fsdp", "trow"), "tcol"),
        ),
        check_vma=False,
    )
```

profile of v0, /device:TPU:0, one launch (start us, length us, event | category | flops | bytes accessed | tf_op | source)
XLA Modules:
  0.0 339.8 jit_solution(15268222778512639576)
XLA Ops:
  7.2 0.0 all-gather.3.cloned.1.call-start
  7.2 1.3 convert_reduce_fusion
  8.5 13.5 %all-reduce.1 = (f32[256]{0:T(256)S(1)}, f32[256]{0:T(256)S(1)}) all-reduce(f32[256]{0:T(256)S(1)} %get-tuple-element.7, f32[256]{0:T(256)S(1)} %get-tuple-element.6), channel_id=1, replica_groups=mesh['fsdp'=2,'trow'=4,'tcol'=4] {'tcol'}, use_global_device_ids=true, to_apply=%region_3.0 | all-reduce | flops 512 | bytes 4096 | tf_op jit(solution)/shard_map/psum | solution.py:27
  22.0 2.1 fusion.16
  24.1 0.0 all-gather.3.cloned.1.call-update
  24.1 0.0 all-gather.5.cloned.1.call-start
  24.2 0.7 all-gather.5.cloned.1.call-update
  24.9 0.0 all-reduce.7.cloned.1.call-start
  24.9 18.8 %all-gather.3.cloned.1.call-done = bf16[512,1024]{1,0:T(8,128)(2,1)} async-done(((bf16[256,1024]{1,0:T(8,128)(2,1)}), bf16[512,1024]{1,0:T(8,128)(2,1)}) %all-gather.3.cloned.1.call-update) | async-done | bytes 1048592 | tf_op jit(solution)/shard_map/all_gather | solution.py:34
  43.8 6.2 %convolution_convert_fusion.3 = bf16[512,2048]{1,0:T(8,128)(2,1)} fusion(bf16[512,1024]{1,0:T(8,128)(2,1)} %all-gather.3.cloned.1.call-done, bf16[1024,2048]{1,0:T(8,128)(2,1)} %param.5), kind=kOutput, calls=%fused_computation.17 | convolution fusion | flops 2148532224 | bytes 7340032 | tf_op jit(solution)/shard_map/dot_general | solution.py:18
  49.9 16.7 %all-gather.5.cloned.1.call-done = bf16[512,1024]{1,0:T(8,128)(2,1)} async-done(((bf16[256,1024]{1,0:T(8,128)(2,1)}), bf16[512,1024]{1,0:T(8,128)(2,1)}) %all-gather.5.cloned.1.call-update) | async-done | bytes 1048592 | tf_op jit(solution)/shard_map/all_gather | solution.py:26
  66.6 6.2 %convolution_convert_fusion.2 = bf16[512,2048]{1,0:T(8,128)(2,1)} fusion(bf16[512,1024]{1,0:T(8,128)(2,1)} %all-gather.5.cloned.1.call-done, bf16[2048,1024]{1,0:T(8,128)(2,1)} %param.6), kind=kOutput, calls=%fused_computation.16 | convolution fusion | flops 2148532224 | bytes 7340032 | tf_op jit(solution)/shard_map/dot_general | solution.py:18
  72.8 0.0 all-reduce.7.cloned.1.call-update
  72.8 0.0 reduce-scatter.5.cloned.1.call-start
  72.9 155.1 %all-reduce.7.cloned.1.call-done = (bf16[512,2048]{1,0:T(8,128)(2,1)}, bf16[512,2048]{1,0:T(8,128)(2,1)}) async-done(((bf16[512,2048]{1,0:T(8,128)(2,1)}, bf16[512,2048]{1,0:T(8,128)(2,1)}), (bf16[512,2048]{1,0:T(8,128)(2,1)}, bf16[512,2048]{1,0:T(8,128)(2,1)})) %all-reduce.7.cloned.1.call-update) | async-done | bytes 4194320 | tf_op jit(solution)/shard_map/psum | solution.py:38
  228.0 0.0 copy-start.4
  228.0 3.7 %fusion.8 = bf16[512,2048]{1,0:T(8,128)(2,1)S(1)} fusion(bf16[512,2048]{1,0:T(8,128)(2,1)} %get-tuple-element.12, bf16[512,2048]{1,0:T(8,128)(2,1)} %get-tuple-element.13), kind=kLoop, calls=%fused_computation.13 | loop fusion | flops 12582912 | bytes 6291456 | tf_op jit(solution)/shard_map/convert_element_type | solution.py:40
  231.7 0.0 copy-start.2
  231.7 1.3 copy-done.2
  233.0 0.0 copy-done.4
  233.0 0.0 copy-start.1
  233.0 3.4 convolution_convert_fusion.4
  236.4 0.0 reduce-scatter.5.cloned.1.call-update
  236.4 0.0 copy-start.5
  236.4 0.0 reduce-scatter.3.cloned.1.call-start
  236.5 0.0 copy-done.1
  236.5 5.7 %convolution_convert_fusion.5 = bf16[512,1024]{1,0:T(8,128)(2,1)} fusion(bf16[2048,1024]{1,0:T(8,128)(2,1)} %param.6, bf16[512,2048]{1,0:T(8,128)(2,1)S(1)} %copy-done.1), kind=kOutput, calls=%fused_computation.26 | convolution fusion | flops 2154299392 | bytes 7340032 | tf_op jit(solution)/shard_map/dot_general | solution.py:18
  242.2 0.0 reduce-scatter.3.cloned.1.call-update
  242.2 0.2 all-reduce.9.cloned.1.call-start
  242.5 0.0 copy-done.5
  242.5 6.0 %convolution_convert_fusion.1 = bf16[1024,2048]{1,0:T(8,128)(2,1)} fusion(bf16[512,1024]{1,0:T(8,128)(2,1)S(1)} %copy-done.5, bf16[512,2048]{1,0:T(8,128)(2,1)} %copy-done.2), kind=kOutput, calls=%fused_computation.15 | convolution fusion | flops 2149580800 | bytes 7340032 | tf_op jit(solution)/shard_map/dot_general | solution.py:18
  248.5 7.5 %reduce-scatter.5.cloned.1.call-done = bf16[256,1024]{1,0:T(8,128)(2,1)} async-done(((bf16[512,1024]{1,0:T(8,128)(2,1)}), bf16[256,1024]{1,0:T(8,128)(2,1)}) %reduce-scatter.5.cloned.1.call-update) | async-done | bytes 524304 | tf_op jit(solution)/shard_map/reduce_scatter | solution.py:46
  256.0 22.5 %reduce-scatter.3.cloned.1.call-done = bf16[256,1024]{1,0:T(8,128)(2,1)} async-done(((bf16[512,1024]{1,0:T(8,128)(2,1)}), bf16[256,1024]{1,0:T(8,128)(2,1)}) %reduce-scatter.3.cloned.1.call-update) | async-done | bytes 524304 | tf_op jit(solution)/shard_map/reduce_scatter | solution.py:41
  278.5 0.0 all-reduce.9.cloned.1.call-update
  278.5 0.0 copy-start
  278.5 0.0 copy-start.3
  278.5 5.4 %convolution_convert_fusion = bf16[2048,1024]{1,0:T(8,128)(2,1)} fusion(bf16[512,1024]{1,0:T(8,128)(2,1)} %all-gather.5.cloned.1.call-done, bf16[512,2048]{1,0:T(8,128)(2,1)S(1)} %copy-done.1), kind=kOutput, calls=%fused_computation.14 | convolution fusion | flops 2155872256 | bytes 7340032 | tf_op jit(solution)/shard_map/dot_general | solution.py:18
  283.9 33.2 %all-reduce.9.cloned.1.call-done = (bf16[256,1024]{1,0:T(8,128)(2,1)}, bf16[256,1024]{1,0:T(8,128)(2,1)}) async-done(((bf16[256,1024]{1,0:T(8,128)(2,1)}, bf16[256,1024]{1,0:T(8,128)(2,1)}), (bf16[256,1024]{1,0:T(8,128)(2,1)}, bf16[256,1024]{1,0:T(8,128)(2,1)})) %all-reduce.9.cloned.1.call-update) | async-done | bytes 1048592 | tf_op jit(solution)/shard_map/psum | solution.py:44
  317.1 0.0 copy-done
  317.1 1.5 convert_reduce_fusion.1
  318.6 11.7 %all-reduce = (f32[256]{0:T(256)S(1)}, f32[256]{0:T(256)S(1)}) all-reduce(f32[256]{0:T(256)S(1)} %get-tuple-element.5, f32[256]{0:T(256)S(1)} %get-tuple-element.4), channel_id=1, replica_groups=mesh['fsdp'=2,'trow'=4,'tcol'=4] {'tcol'}, use_global_device_ids=true, to_apply=%region_13.0 | all-reduce | flops 512 | bytes 4096 | tf_op jit(solution)/shard_map/psum | solution.py:52
  330.3 0.0 copy-done.3
  330.3 2.6 fusion.12
  (2 shorter events, 0.0 us)
Async XLA Ops:
  7.2 36.6 %all-gather.3.cloned.1.call-start = ((), (), s32[]{:S(2)}) async-start(), calls=%async_computation.2 | async-start | bytes 1572864 | tf_op jit(solution)/shard_map/all_gather | solution.py:34
  24.1 42.5 %all-gather.5.cloned.1.call-start = ((), (), s32[]{:S(2)}) async-start(), calls=%async_computation.4 | async-start | bytes 1572864 | tf_op jit(solution)/shard_map/all_gather | solution.py:26
  24.9 203.1 %all-reduce.7.cloned.1.call-start = ((), (), s32[]{:S(2)}) async-start(), calls=%async_computation.6 | async-start | bytes 8388608 | tf_op jit(solution)/shard_map/psum | solution.py:38
  72.8 183.1 %reduce-scatter.5.cloned.1.call-start = ((), (), s32[]{:S(2)}) async-start(), calls=%async_computation.5 | async-start | bytes 1572864 | tf_op jit(solution)/shard_map/reduce_scatter | solution.py:46
  228.0 5.0 %copy-start.4 = (bf16[1024,2048]{1,0:T(8,128)(2,1)S(1)}, bf16[1024,2048]{1,0:T(8,128)(2,1)}, u32[]{:S(2)}) copy-start(bf16[1024,2048]{1,0:T(8,128)(2,1)} %param.5) | copy-start | bytes 12582916
  231.7 1.3 copy-start.2
  233.0 3.4 %copy-start.1 = (bf16[512,2048]{1,0:T(8,128)(2,1)S(1)}, bf16[512,2048]{1,0:T(8,128)(2,1)}, u32[]{:S(2)}) copy-start(bf16[512,2048]{1,0:T(8,128)(2,1)} %get-tuple-element.12) | copy-start | bytes 6291460
  236.4 6.1 %copy-start.5 = (bf16[512,1024]{1,0:T(8,128)(2,1)S(1)}, bf16[512,1024]{1,0:T(8,128)(2,1)}, u32[]{:S(2)}) copy-start(bf16[512,1024]{1,0:T(8,128)(2,1)} %all-gather.3.cloned.1.call-done) | copy-start | bytes 3145732
  236.4 42.0 %reduce-scatter.3.cloned.1.call-start = ((), (), s32[]{:S(2)}) async-start(), calls=%async_computation.3 | async-start | bytes 1572864 | tf_op jit(solution)/shard_map/reduce_scatter | solution.py:41
  242.2 74.9 %all-reduce.9.cloned.1.call-start = ((), (), s32[]{:S(2)}) async-start(), calls=%async_computation.7 | async-start | bytes 2097152 | tf_op jit(solution)/shard_map/psum | solution.py:44
  278.5 38.6 %copy-start = (bf16[256,1024]{1,0:T(8,128)(2,1)S(1)}, bf16[256,1024]{1,0:T(8,128)(2,1)}, u32[]{:S(2)}) copy-start(bf16[256,1024]{1,0:T(8,128)(2,1)} %param.4) | copy-start | bytes 1572868
  278.5 51.8 %copy-start.3 = (bf16[256,1024]{1,0:T(8,128)(2,1)S(1)}, bf16[256,1024]{1,0:T(8,128)(2,1)}, u32[]{:S(2)}) copy-start(bf16[256,1024]{1,0:T(8,128)(2,1)} %param.7) | copy-start | bytes 1572868
Sparse Core Ops, SparseCore 0:
  24.2 19.4 all-gather.2
  45.3 21.2 all-gather.4
  73.0 155.0 all-reduce.6
  236.5 19.3 reduce-scatter.4
  258.0 20.3 reduce-scatter.2
  280.8 36.3 all-reduce.8
where the time goes:
time: 340 us
  waiting for transfers between devices  255 us (75%)
  matrix products  32.8 us (10%)
  blocking collectives  25.2 us (7%)
  between operations  14.2 us (4%)
  other arithmetic  11.2 us (3%)
    psum x1, waiting for transfers between devices, local(): lax.psum(contract(normed, w_up, 1, 0).astype(jnp.bfloat16), 'tcol')  155 us
    psum x1, waiting for transfers between devices, local(): branch = lax.psum(branch, 'trow').astype(jnp.float32)  33.2 us
    dot_general x6, matrix products, contract(): lax.dot_general(left, right, (((left_dim,), (right_dim,)), ((), ())), pre...  32.8 us
    reduce_scatter x1, waiting for transfers between devices, local(): lax.psum_scatter(contract(hidden, w_down, 1, 0).astype(jnp.bfloat16), 'fs...  22.5 us
    all_gather x1, waiting for transfers between devices, local(): lax.all_gather(centered_scaled.astype(jnp.bfloat16), 'fsdp', axis=0, tile...  18.8 us
    all_gather x1, waiting for transfers between devices, local(): cot_all = lax.all_gather(cotangent, 'fsdp', axis=0, tiled=True)  16.7 us
    psum x1, blocking collectives, local(): lax.psum((jnp.sum(input_float, axis=1), jnp.sum(input_float * input_float...  13.5 us
    psum x1, blocking collectives, local(): lax.psum((jnp.sum(dnorm, axis=1), jnp.sum(dnorm * centered_scaled, axis=1...  11.7 us
  transfers between devices with their start and end apart: 6, of which 6 were waited for; matrix products, arithmetic and copies ran while one was open for 7% of the time, Pallas kernels for 0%

commit v1 on v0

--- a/solution.py
+++ b/solution.py
@@ -41,7 +41,7 @@
     branch = lax.psum_scatter(
         contract(hidden, w_down, 1, 0).astype(jnp.bfloat16), "fsdp", scatter_dimension=0, tiled=True
     )
-    branch = lax.psum(branch, "trow").astype(jnp.float32)
+    branch = lax.all_gather(branch, axis_name="trow").sum(axis=0).astype(jnp.float32)
     mixed = (input_float + branch).astype(jnp.bfloat16)
     dnorm = lax.psum_scatter(
         contract(dpre, w_up, 1, 1).astype(jnp.bfloat16), "fsdp", scatter_dimension=0, tiled=True

time: 340 us -> 350 us (1.029)
  waiting for transfers between devices: 255 us -> 264 us
    all_gather x0 -> x1, waiting for transfers between devices: none -> 11.1 us  [local(): lax.all_gather(branch, axis_name='trow').sum(axis=0).astype(jnp.float32)]
    psum x1, waiting for transfers between devices: 33.2 us -> 25.4 us  [local(): dnorm = lax.psum(dnorm, 'trow').astype(jnp.float32)]
    reduce_scatter x1, waiting for transfers between devices: 7.45 us -> 13.7 us  [local(): lax.psum_scatter(contract(dpre, w_up, 1, 1).astype(jnp.bfloat16), 'fsdp',...]
  transfers between devices with their start and end apart: 6 -> 7, of which waited for: 6 -> 7; matrix products, arithmetic and copies ran while one was open for 7% -> 7% of each run, Pallas kernels for 0% -> 0%
where the time goes in v1:
time: 350 us
  waiting for transfers between devices  264 us (75%)
  matrix products  31.6 us (9%)
  blocking collectives  25.2 us (7%)
  between operations  14.2 us (4%)
  other arithmetic  13 us (4%)
    psum x1, waiting for transfers between devices, local(): lax.psum(contract(normed, w_up, 1, 0).astype(jnp.bfloat16), 'tcol')  155 us
    dot_general x6, matrix products, contract(): lax.dot_general(left, right, (((left_dim,), (right_dim,)), ((), ())), pre...  31.6 us
    psum x1, waiting for transfers between devices, local(): dnorm = lax.psum(dnorm, 'trow').astype(jnp.float32)  25.4 us
    reduce_scatter x1, waiting for transfers between devices, local(): lax.psum_scatter(contract(hidden, w_down, 1, 0).astype(jnp.bfloat16), 'fs...  22.3 us
    all_gather x1, waiting for transfers between devices, local(): lax.all_gather(centered_scaled.astype(jnp.bfloat16), 'fsdp', axis=0, tile...  18.8 us
    all_gather x1, waiting for transfers between devices, local(): cot_all = lax.all_gather(cotangent, 'fsdp', axis=0, tiled=True)  16.7 us
    reduce_scatter x1, waiting for transfers between devices, local(): lax.psum_scatter(contract(dpre, w_up, 1, 1).astype(jnp.bfloat16), 'fsdp',...  13.7 us
    psum x1, blocking collectives, local(): lax.psum((jnp.sum(input_float, axis=1), jnp.sum(input_float * input_float...  13.5 us
  transfers between devices with their start and end apart: 7, of which 7 were waited for; matrix products, arithmetic and copies ran while one was open for 7% of the time, Pallas kernels for 0%

profile of v1, /device:TPU:0, one launch (start us, length us, event | category | flops | bytes accessed | tf_op | source)
XLA Modules:
  0.0 349.7 jit_solution(11202939882354797309)
XLA Ops:
  7.2 0.0 all-gather.5.cloned.1.call-start
  7.2 1.3 convert_reduce_fusion
  8.5 13.5 %all-reduce.1 = (f32[256]{0:T(256)S(1)}, f32[256]{0:T(256)S(1)}) all-reduce(f32[256]{0:T(256)S(1)} %get-tuple-element.7, f32[256]{0:T(256)S(1)} %get-tuple-element.6), channel_id=1, replica_groups=mesh['fsdp'=2,'trow'=4,'tcol'=4] {'tcol'}, use_global_device_ids=true, to_apply=%region_3.0 | all-reduce | flops 512 | bytes 4096 | tf_op jit(solution)/shard_map/psum | solution.py:27
  22.0 2.1 fusion.16
  24.1 0.0 all-gather.5.cloned.1.call-update
  24.1 0.0 all-gather.7.cloned.1.call-start
  24.2 0.7 all-gather.7.cloned.1.call-update
  24.9 0.0 all-reduce.8.cloned.1.call-start
  24.9 18.8 %all-gather.5.cloned.1.call-done = bf16[512,1024]{1,0:T(8,128)(2,1)} async-done(((bf16[256,1024]{1,0:T(8,128)(2,1)}), bf16[512,1024]{1,0:T(8,128)(2,1)}) %all-gather.5.cloned.1.call-update) | async-done | bytes 1048592 | tf_op jit(solution)/shard_map/all_gather | solution.py:34
  43.8 6.2 %convolution_convert_fusion.3 = bf16[512,2048]{1,0:T(8,128)(2,1)} fusion(bf16[512,1024]{1,0:T(8,128)(2,1)} %all-gather.5.cloned.1.call-done, bf16[1024,2048]{1,0:T(8,128)(2,1)} %param.5), kind=kOutput, calls=%fused_computation.17 | convolution fusion | flops 2148532224 | bytes 7340032 | tf_op jit(solution)/shard_map/dot_general | solution.py:18
  49.9 16.7 %all-gather.7.cloned.1.call-done = bf16[512,1024]{1,0:T(8,128)(2,1)} async-done(((bf16[256,1024]{1,0:T(8,128)(2,1)}), bf16[512,1024]{1,0:T(8,128)(2,1)}) %all-gather.7.cloned.1.call-update) | async-done | bytes 1048592 | tf_op jit(solution)/shard_map/all_gather | solution.py:26
  66.6 6.2 %convolution_convert_fusion.2 = bf16[512,2048]{1,0:T(8,128)(2,1)} fusion(bf16[512,1024]{1,0:T(8,128)(2,1)} %all-gather.7.cloned.1.call-done, bf16[2048,1024]{1,0:T(8,128)(2,1)} %param.6), kind=kOutput, calls=%fused_computation.16 | convolution fusion | flops 2148532224 | bytes 7340032 | tf_op jit(solution)/shard_map/dot_general | solution.py:18
  72.8 0.0 all-reduce.8.cloned.1.call-update
  72.8 0.0 reduce-scatter.5.cloned.1.call-start
  72.9 155.1 %all-reduce.8.cloned.1.call-done = (bf16[512,2048]{1,0:T(8,128)(2,1)}, bf16[512,2048]{1,0:T(8,128)(2,1)}) async-done(((bf16[512,2048]{1,0:T(8,128)(2,1)}, bf16[512,2048]{1,0:T(8,128)(2,1)}), (bf16[512,2048]{1,0:T(8,128)(2,1)}, bf16[512,2048]{1,0:T(8,128)(2,1)})) %all-reduce.8.cloned.1.call-update) | async-done | bytes 4194320 | tf_op jit(solution)/shard_map/psum | solution.py:38
  228.0 0.0 copy-start.4
  228.0 3.7 %fusion.8 = bf16[512,2048]{1,0:T(8,128)(2,1)S(1)} fusion(bf16[512,2048]{1,0:T(8,128)(2,1)} %get-tuple-element.12, bf16[512,2048]{1,0:T(8,128)(2,1)} %get-tuple-element.13), kind=kLoop, calls=%fused_computation.13 | loop fusion | flops 12582912 | bytes 6291456 | tf_op jit(solution)/shard_map/convert_element_type | solution.py:40
  231.7 0.0 copy-start.2
  231.7 1.3 copy-done.2
  233.0 0.0 copy-done.4
  233.0 0.0 copy-start.1
  233.0 3.4 convolution_convert_fusion.4
  236.4 0.0 reduce-scatter.5.cloned.1.call-update
  236.4 0.0 copy-start.5
  236.4 0.0 reduce-scatter.3.cloned.1.call-start
  236.5 0.0 copy-done.1
  236.5 5.7 %convolution_convert_fusion.5 = bf16[512,1024]{1,0:T(8,128)(2,1)} fusion(bf16[2048,1024]{1,0:T(8,128)(2,1)} %param.6, bf16[512,2048]{1,0:T(8,128)(2,1)S(1)} %copy-done.1), kind=kOutput, calls=%fused_computation.26 | convolution fusion | flops 2154299392 | bytes 7340032 | tf_op jit(solution)/shard_map/dot_general | solution.py:18
  242.2 0.0 reduce-scatter.3.cloned.1.call-update
  242.2 0.0 all-reduce.6.cloned.1.call-start
  242.3 13.7 %reduce-scatter.5.cloned.1.call-done = bf16[256,1024]{1,0:T(8,128)(2,1)} async-done(((bf16[512,1024]{1,0:T(8,128)(2,1)}), bf16[256,1024]{1,0:T(8,128)(2,1)}) %reduce-scatter.5.cloned.1.call-update) | async-done | bytes 524304 | tf_op jit(solution)/shard_map/reduce_scatter | solution.py:46
  255.9 0.0 all-reduce.6.cloned.1.call-update
  256.0 0.2 all-gather.9.cloned.1.call-start
  256.2 22.3 %reduce-scatter.3.cloned.1.call-done = bf16[256,1024]{1,0:T(8,128)(2,1)} async-done(((bf16[512,1024]{1,0:T(8,128)(2,1)}), bf16[256,1024]{1,0:T(8,128)(2,1)}) %reduce-scatter.3.cloned.1.call-update) | async-done | bytes 524304 | tf_op jit(solution)/shard_map/reduce_scatter | solution.py:41
  278.5 0.0 all-gather.9.cloned.1.call-update
  278.5 0.0 copy-done.5
  278.5 0.0 copy-start.6
  278.5 6.1 %convolution_convert_fusion.1 = bf16[1024,2048]{1,0:T(8,128)(2,1)} fusion(bf16[512,1024]{1,0:T(8,128)(2,1)S(1)} %copy-done.5, bf16[512,2048]{1,0:T(8,128)(2,1)} %copy-done.2), kind=kOutput, calls=%fused_computation.15 | convolution fusion | flops 2149580800 | bytes 7340032 | tf_op jit(solution)/shard_map/dot_general | solution.py:18
  284.6 0.0 copy-done.6
  284.6 0.0 copy-start
  284.6 0.0 copy-start.3
  284.6 4.0 %convolution_convert_fusion = bf16[2048,1024]{1,0:T(8,128)(2,1)} fusion(bf16[512,1024]{1,0:T(8,128)(2,1)S(1)} %copy-done.6, bf16[512,2048]{1,0:T(8,128)(2,1)S(1)} %copy-done.1), kind=kOutput, calls=%fused_computation.14 | convolution fusion | flops 2155872256 | bytes 7340032 | tf_op jit(solution)/shard_map/dot_general | solution.py:18
  288.6 25.4 %all-reduce.6.cloned.1.call-done = bf16[256,1024]{1,0:T(8,128)(2,1)} async-done(((bf16[256,1024]{1,0:T(8,128)(2,1)}), bf16[256,1024]{1,0:T(8,128)(2,1)}) %all-reduce.6.cloned.1.call-update) | async-done | bytes 524304 | tf_op jit(solution)/shard_map/psum | solution.py:49
  314.1 0.0 copy-done
  314.1 1.5 convert_reduce_fusion.1
  315.6 11.7 %all-reduce = (f32[256]{0:T(256)S(1)}, f32[256]{0:T(256)S(1)}) all-reduce(f32[256]{0:T(256)S(1)} %get-tuple-element.5, f32[256]{0:T(256)S(1)} %get-tuple-element.4), channel_id=1, replica_groups=mesh['fsdp'=2,'trow'=4,'tcol'=4] {'tcol'}, use_global_device_ids=true, to_apply=%region_13.0 | all-reduce | flops 512 | bytes 4096 | tf_op jit(solution)/shard_map/psum | solution.py:52
  327.3 11.1 %all-gather.9.cloned.1.call-done = bf16[1024,1024]{1,0:T(8,128)(2,1)} async-done(((bf16[256,1024]{1,0:T(8,128)(2,1)}), bf16[1024,1024]{1,0:T(8,128)(2,1)}) %all-gather.9.cloned.1.call-update) | async-done | bytes 2097168 | tf_op jit(solution)/shard_map/all_gather | solution.py:44
  338.4 2.0 reduce_sum.50
  340.4 0.0 copy-done.3
  340.4 2.4 fusion.12
  (2 shorter events, 0.0 us)
Async XLA Ops:
  7.2 36.6 %all-gather.5.cloned.1.call-start = ((), (), s32[]{:S(2)}) async-start(), calls=%async_computation.2 | async-start | bytes 1572864 | tf_op jit(solution)/shard_map/all_gather | solution.py:34
  24.1 42.5 %all-gather.7.cloned.1.call-start = ((), (), s32[]{:S(2)}) async-start(), calls=%async_computation.4 | async-start | bytes 1572864 | tf_op jit(solution)/shard_map/all_gather | solution.py:26
  24.9 203.1 %all-reduce.8.cloned.1.call-start = ((), (), s32[]{:S(2)}) async-start(), calls=%async_computation.8 | async-start | bytes 8388608 | tf_op jit(solution)/shard_map/psum | solution.py:38
  72.8 183.1 %reduce-scatter.5.cloned.1.call-start = ((), (), s32[]{:S(2)}) async-start(), calls=%async_computation.5 | async-start | bytes 1572864 | tf_op jit(solution)/shard_map/reduce_scatter | solution.py:46
  228.0 5.0 %copy-start.4 = (bf16[1024,2048]{1,0:T(8,128)(2,1)S(1)}, bf16[1024,2048]{1,0:T(8,128)(2,1)}, u32[]{:S(2)}) copy-start(bf16[1024,2048]{1,0:T(8,128)(2,1)} %param.5) | copy-start | bytes 12582916
  231.7 1.3 copy-start.2
  233.0 3.4 copy-start.1
  236.4 42.1 %copy-start.5 = (bf16[512,1024]{1,0:T(8,128)(2,1)S(1)}, bf16[512,1024]{1,0:T(8,128)(2,1)}, u32[]{:S(2)}) copy-start(bf16[512,1024]{1,0:T(8,128)(2,1)} %all-gather.5.cloned.1.call-done) | copy-start | bytes 3145732
  236.4 42.0 %reduce-scatter.3.cloned.1.call-start = ((), (), s32[]{:S(2)}) async-start(), calls=%async_computation.3 | async-start | bytes 1572864 | tf_op jit(solution)/shard_map/reduce_scatter | solution.py:41
  242.2 71.9 %all-reduce.6.cloned.1.call-start = ((), (), s32[]{:S(2)}) async-start(), calls=%async_computation.6 | async-start | bytes 1048576 | tf_op jit(solution)/shard_map/psum | solution.py:49
  256.0 82.4 %all-gather.9.cloned.1.call-start = ((), (), s32[]{:S(2)}) async-start(), calls=%async_computation.7 | async-start | bytes 2621440 | tf_op jit(solution)/shard_map/all_gather | solution.py:44
  278.5 6.1 %copy-start.6 = (bf16[512,1024]{1,0:T(8,128)(2,1)S(1)}, bf16[512,1024]{1,0:T(8,128)(2,1)}, u32[]{:S(2)}) copy-start(bf16[512,1024]{1,0:T(8,128)(2,1)} %all-gather.7.cloned.1.call-done) | copy-start | bytes 3145732
  284.6 29.5 %copy-start = (bf16[256,1024]{1,0:T(8,128)(2,1)S(1)}, bf16[256,1024]{1,0:T(8,128)(2,1)}, u32[]{:S(2)}) copy-start(bf16[256,1024]{1,0:T(8,128)(2,1)} %param.4) | copy-start | bytes 1572868
  284.6 55.8 %copy-start.3 = (bf16[256,1024]{1,0:T(8,128)(2,1)S(1)}, bf16[256,1024]{1,0:T(8,128)(2,1)}, u32[]{:S(2)}) copy-start(bf16[256,1024]{1,0:T(8,128)(2,1)} %param.7) | copy-start | bytes 1572868
Sparse Core Ops, SparseCore 0:
  24.2 19.4 all-gather.4
  45.3 21.2 all-gather.6
  73.0 155.0 all-reduce.7
  236.5 19.3 reduce-scatter.4
  258.0 20.3 reduce-scatter.2
  280.7 33.3 all-reduce.5
  315.6 22.6 all-gather.8
